TPU v7x, 32 devices: a whole 2x2x4 slice. The times are simulated.
32 devices in a mesh: row: 8 (over z, y), col: 4 (over x, core).
Axes of the slice: x: 2, y: 2, z: 4, core: 2. Of those that a mesh axis runs over, the one named last changes fastest.
Arguments:
- tile_values: bfloat16 [128, 8, 256, 256], P(('row', 'col')), may hold values from -0.375 to 0.375
- block_columns: int32 [128, 8], P(('row', 'col')), may hold values from 0 to 127, as said below
- tile_counts: int32 [128], P(('row', 'col')), may hold values from 1 to 8, as said below
- diagonal: float32 [32768], P(('row', 'col')), may hold values from 0.5 to 4
- sketch_rows: int32 [32768], P(('row', 'col')), may hold values from 0 to 1023
- sketch_signs: int32 [32768], P(('row', 'col')), may hold values from 0 to 1
- right_side: float32 [16, 32768], P(None, ('row', 'col')), may hold values from -70 to 70
Outputs:
- solution: float32 [16, 32768], P(None, ('row', 'col'))
- last_basis: float32 [16, 32768], P(None, ('row', 'col'))
- hessenberg: float32 [16, 5, 4], replicated
Inputs may be any that keep to these rules, and one draw needn't show every extreme that they name: `block_columns`: for block row b all 8 entries are distinct block columns c with (c - b) mod 128 <= 4 or >= 124; only slots k < tile_counts[b] are used. `tile_counts`: in every draw the 4 block rows of at least one device all have 8.
All inputs are finite; a program needn't handle non-finite values.
Results may differ from a plain program's by a relative error of at most 0.0053.
Values may be sent and summed in bfloat16 or wider, within the bound.
A program may use at most 64 MiB of HBM per device.

v0:
```python
import math

import jax
import jax.numpy as jnp
from jax import lax
from jax.sharding import PartitionSpec as P

SKETCH = 1024
ITERS = 4


epsilon = 1e-06
highest = lax.Precision.HIGHEST


def with_halo(block, sides, width):
    for axis, dim in sides:
        count = lax.axis_size(axis)
        forward = [(i, i + 1) for i in range(count - 1)]
        forward.append((count - 1, 0))
        backward = [(target, source) for source, target in forward]
        low = lax.ppermute(
            lax.slice_in_dim(block, block.shape[dim] - width, None, axis=dim), axis, forward
        )
        high = lax.ppermute(lax.slice_in_dim(block, 0, width, axis=dim), axis, backward)
        block = jnp.concatenate([low, block, high], axis=dim)
    return block


def cholesky_solve(gram, target):
    order = gram.shape[1]
    factor = {}
    for column in range(order):
        diag_part = gram[:, column, column]
        for inner in range(column):
            diag_part = diag_part - factor[column, inner] * factor[column, inner]
        factor[column, column] = jnp.sqrt(diag_part)
        for below in range(column + 1, order):
            entry = gram[:, below, column]
            for inner in range(column):
                entry = entry - factor[below, inner] * factor[column, inner]
            factor[below, column] = entry / factor[column, column]
    forward = []
    for column in range(order):
        entry = target[:, column]
        for inner in range(column):
            entry = entry - factor[column, inner] * forward[inner]
        forward.append(entry / factor[column, column])
    result = [None] * order
    for column in reversed(range(order)):
        entry = forward[column]
        for inner in range(column + 1, order):
            entry = entry - factor[inner, column] * result[inner]
        result[column] = entry / factor[column, column]
    return jnp.stack(result, axis=1)


def sketch_solve(stacked, image_sketch):
    gram = jnp.einsum("rjk,rmk->rjm", stacked, stacked, precision=highest)
    target = jnp.einsum("rjk,rk->rj", stacked, image_sketch, precision=highest)
    return cholesky_solve(gram, target)


def local(tile_values, block_columns, tile_counts, diagonal, sketch_rows, sketch_signs, right_side):
    col_count = lax.axis_size("col")
    devices = lax.axis_size("row") * col_count
    device_index = lax.axis_index("row") * col_count + lax.axis_index("col")
    block_rows = tile_values.shape[0]
    slot_count = tile_values.shape[1]
    tile_size = tile_values.shape[2]
    systems = right_side.shape[0]
    all_blocks = block_rows * devices
    scaling = 1.0 / math.sqrt(all_blocks * tile_size)
    signed = (2 * sketch_signs - 1).astype(jnp.float32) * scaling
    projector = jnp.where(sketch_rows[:, None] == jnp.arange(SKETCH)[None, :], signed[:, None], 0.0)
    live_mask = jnp.arange(slot_count)[None, :] < tile_counts[:, None]
    first_block = device_index * block_rows
    turns = jnp.max(jnp.sum(live_mask.astype(jnp.int32), axis=1))
    live_weight = live_mask.astype(jnp.float32)
    start = lax.psum(jnp.dot(right_side, projector, precision=highest), ("row", "col"))
    beta = jnp.sqrt(jnp.sum(start * start, axis=1) + epsilon)
    basis = [right_side / beta[:, None]]
    sketched = [start / beta[:, None]]
    columns_list = []
    for step_index in range(ITERS):
        vector = basis[-1]
        shadow = vector.astype(jnp.bfloat16)
        widened = with_halo(shadow, ((("row", "col"), 1),), block_rows * tile_size)
        start_block = first_block - block_rows
        blocks = widened.reshape(systems, widened.shape[1] // tile_size, tile_size)
        local_index = (block_columns - start_block) % all_blocks

        def add_slot(slot_turn, running):
            slot_tiles = lax.dynamic_index_in_dim(tile_values, slot_turn, 1, keepdims=False)
            wanted = lax.dynamic_index_in_dim(local_index, slot_turn, 1, keepdims=False)
            picked = jnp.take(blocks, wanted, axis=1)
            weight_mask = lax.dynamic_index_in_dim(live_weight, slot_turn, 1, keepdims=False)
            product = jnp.einsum(
                "rbi,boi->rbo", picked, slot_tiles, preferred_element_type=jnp.float32
            )
            return running + product * weight_mask[None, :, None]

        tile_sum = lax.fori_loop(
            0, turns, add_slot, jnp.zeros((systems, block_rows, tile_size), jnp.float32)
        )
        image = diagonal[None, :] * vector + tile_sum.reshape(systems, block_rows * tile_size)
        image_sketch = lax.psum(jnp.dot(image, projector, precision=highest), ("row", "col"))
        stacked = jnp.stack(sketched, axis=1)
        coeffs = sketch_solve(stacked, image_sketch)
        fresh = image - jnp.einsum(
            "rj,rjn->rn", coeffs, jnp.stack(basis, axis=1), precision=highest
        )
        fresh_sketch = image_sketch - jnp.einsum("rj,rjk->rk", coeffs, stacked, precision=highest)
        norm_new = jnp.sqrt(jnp.sum(fresh_sketch * fresh_sketch, axis=1) + epsilon)
        basis.append(fresh / norm_new[:, None])
        sketched.append(fresh_sketch / norm_new[:, None])
        padding = jnp.zeros((systems, ITERS - step_index - 1), jnp.float32)
        columns_list.append(jnp.concatenate([coeffs, norm_new[:, None], padding], axis=1))
    hessenberg = jnp.stack(columns_list, axis=2)
    gram = jnp.einsum("rim,rin->rmn", hessenberg, hessenberg, precision=highest)
    weights = cholesky_solve(gram, beta[:, None] * hessenberg[:, 0, :])
    solution = jnp.einsum(
        "rm,rmn->rn", weights, jnp.stack(basis[:ITERS], axis=1), precision=highest
    )
    return (solution, basis[-1], hessenberg)


def solution(mesh):
    in_specs = (
        P(("row", "col"), None, None, None),
        P(("row", "col"), None),
        P(("row", "col")),
        P(("row", "col")),
        P(("row", "col")),
        P(("row", "col")),
        P(None, ("row", "col")),
    )
    out_specs = (P(None, ("row", "col")), P(None, ("row", "col")), P())
    return jax.shard_map(local, mesh=mesh, in_specs=in_specs, out_specs=out_specs, check_vma=False)
```

profile of v0, /device:TPU:1, one launch (start us, length us, event | category | flops | bytes accessed | tf_op | source)
XLA Modules:
  0.0 768.6 jit_solution(5249777427383235755)
XLA Ops:
  7.9 4.2 fusion.73
  13.6 123.9 %all-reduce.6.cloned.1.call-done = f32[16,1024]{1,0:T(8,128)} async-done(((f32[16,1024]{1,0:T(8,128)}), f32[16,1024]{1,0:T(8,128)}) %all-reduce.6.cloned.1.call-update) | async-done | bytes 65552 | tf_op jit(solution)/shard_map/psum | solution.py:80
  139.5 1.7 collective-permute-start
  141.9 4.5 copy.86
  147.1 21.3 %while.40 = (s32[]{:T(128)}, f32[16,4,256]{2,0,1:T(8,128)S(1)}, s32[]{:T(128)}, bf16[4,8,256,256]{3,2,0,1:T(8,128)(2,1)}, s32[4,8]{0,1:T(8,128)S(1)}, /*index=5*...) while((s32[]{:T(128)}, f32[16,4,256]{2,0,1:T(8,128)S(1)}, ...), condition=%wide.region_5.7_spmd, body=%wide.region_4.6_spmd.sunk | while | flops 8438813 | bytes 758035 | solution.py:103
  148.4 1.3 fusion.184
  151.0 1.3 fusion.184
  153.6 1.3 fusion.184
  156.2 1.3 fusion.184
  158.8 1.3 fusion.184
  161.3 1.3 fusion.184
  163.9 1.3 fusion.184
  166.5 1.3 fusion.184
  168.5 3.2 fusion.54
  171.9 120.5 %all-reduce.8.cloned.1.call-done = f32[16,1024]{1,0:T(8,128)} async-done(((f32[16,1024]{1,0:T(8,128)}), f32[16,1024]{1,0:T(8,128)}) %all-reduce.8.cloned.1.call-update) | async-done | bytes 65552 | tf_op jit(solution)/shard_map/psum | solution.py:107
  292.4 1.0 multiply_reduce_fusion
  293.5 1.1 fusion.147
  295.6 1.7 collective-permute-start.2
  297.3 1.1 fusion.100
  298.9 1.6 collective-permute-done.2
  300.5 21.3 %while.41 = (s32[]{:T(128)}, f32[16,4,256]{2,0,1:T(8,128)S(1)}, s32[]{:T(128)}, bf16[4,8,256,256]{3,2,0,1:T(8,128)(2,1)}, s32[4,8]{0,1:T(8,128)S(1)}, /*index=5*...) while((s32[]{:T(128)}, f32[16,4,256]{2,0,1:T(8,128)S(1)}, ...), condition=%wide.region_9.11_spmd, body=%wide.region_8.10_spmd.sunk | while | flops 8438813 | bytes 758035 | solution.py:103
  301.8 1.3 fusion.188
  304.4 1.3 fusion.188
  307.0 1.3 fusion.188
  309.6 1.3 fusion.188
  312.1 1.3 fusion.188
  314.7 1.3 fusion.188
  317.3 1.3 fusion.188
  319.9 1.3 fusion.188
  321.9 3.1 fusion.52
  325.4 119.0 %all-reduce.10.cloned.1.call-done = f32[16,1024]{1,0:T(8,128)} async-done(((f32[16,1024]{1,0:T(8,128)}), f32[16,1024]{1,0:T(8,128)}) %all-reduce.10.cloned.1.call-update) | async-done | bytes 65552 | tf_op jit(solution)/shard_map/psum | solution.py:107
  444.4 2.0 fusion.98
  447.2 1.0 multiply_reduce_fusion.3
  449.8 1.7 collective-permute-start.4
  451.6 1.2 fusion.80
  453.2 1.5 collective-permute-done.4
  454.8 21.3 %while.42 = (s32[]{:T(128)}, f32[16,4,256]{2,0,1:T(8,128)S(1)}, s32[]{:T(128)}, bf16[4,8,256,256]{3,2,0,1:T(8,128)(2,1)}, s32[4,8]{0,1:T(8,128)S(1)}, /*index=5*...) while((s32[]{:T(128)}, f32[16,4,256]{2,0,1:T(8,128)S(1)}, ...), condition=%wide.region_13.15_spmd, body=%wide.region_12.14_spmd.sunk | while | flops 8438813 | bytes 758035 | solution.py:103
  456.1 1.3 fusion.192
  458.7 1.3 fusion.192
  461.2 1.3 fusion.192
  463.8 1.3 fusion.192
  466.4 1.3 fusion.192
  469.0 1.3 fusion.192
  471.6 1.3 fusion.192
  474.2 1.3 fusion.192
  476.2 3.1 fusion.50
  479.5 119.2 %all-reduce.12.cloned.1.call-done = f32[16,1024]{1,0:T(8,128)} async-done(((f32[16,1024]{1,0:T(8,128)}), f32[16,1024]{1,0:T(8,128)}) %all-reduce.12.cloned.1.call-update) | async-done | bytes 65552 | tf_op jit(solution)/shard_map/psum | solution.py:107
  598.7 2.0 fusion.78
  601.6 1.0 multiply_reduce_fusion.2
  604.2 1.7 collective-permute-start.6
  606.0 1.2 fusion.92
  607.7 1.4 collective-permute-done.6
  609.2 21.6 %while.43 = (s32[]{:T(128)}, f32[16,4,256]{2,0,1:T(8,128)S(1)}, s32[]{:T(128)}, bf16[4,8,256,256]{3,2,0,1:T(8,128)(2,1)}, s32[4,8]{0,1:T(8,128)S(1)}, /*index=5*...) while((s32[]{:T(128)}, f32[16,4,256]{2,0,1:T(8,128)S(1)}, ...), condition=%wide.region_17.19_spmd, body=%wide.region_16.18_spmd.sunk | while | flops 8438813 | bytes 758035 | solution.py:103
  610.5 1.3 fusion.196
  613.0 1.3 fusion.196
  615.6 1.3 fusion.196
  618.2 1.3 fusion.196
  620.8 1.3 fusion.196
  623.4 1.3 fusion.196
  626.0 1.3 fusion.196
  628.6 1.3 fusion.196
  630.8 3.1 fusion.48
  634.1 119.3 %all-reduce.14.cloned.1.call-done = f32[16,1024]{1,0:T(8,128)} async-done(((f32[16,1024]{1,0:T(8,128)}), f32[16,1024]{1,0:T(8,128)}) %all-reduce.14.cloned.1.call-update) | async-done | bytes 65552 | tf_op jit(solution)/shard_map/psum | solution.py:107
  753.4 2.1 fusion.90
  (243 shorter events, 39.0 us)
Async XLA Ops:
  7.2 130.4 %all-reduce.6.cloned.1.call-start = ((), (), s32[]{:S(2)}) async-start(), calls=%async_computation | async-start | bytes 131072 | tf_op jit(solution)/shard_map/psum | solution.py:80
  12.1 280.3 %all-reduce.8.cloned.1.call-start = ((), (), s32[]{:S(2)}) async-start(), calls=%async_computation.1 | async-start | bytes 131072 | tf_op jit(solution)/shard_map/psum | solution.py:107
  139.4 7.7 collective-permute-start.1
  139.5 7.6 collective-permute-start
  146.4 22.1 %copy-start.1 = (f32[16,1024]{1,0:T(8,128)S(1)}, f32[16,1024]{1,0:T(8,128)}, u32[]{:S(2)}) copy-start(f32[16,1024]{1,0:T(8,128)} %param.23) | copy-start | bytes 196612
  146.4 22.1 %copy-start.2 = (f32[1024]{0:T(1024)S(1)}, f32[1024]{0:T(1024)}, u32[]{:S(2)}) copy-start(f32[1024]{0:T(1024)} %param.20) | copy-start | bytes 12292
  146.4 22.1 %copy-start.3 = (s32[1024]{0:T(1024)S(1)}, s32[1024]{0:T(1024)}, u32[]{:S(2)}) copy-start(s32[1024]{0:T(1024)} %param.21) | copy-start | bytes 12292
  146.4 146.0 %copy-start = (f32[16,1024]{1,0:T(8,128)S(1)}, f32[16,1024]{1,0:T(8,128)}, u32[]{:S(2)}) copy-start(f32[16,1024]{1,0:T(8,128)} %all-reduce.6.cloned.1.call-done) | copy-start | bytes 196612
  171.7 272.7 %all-reduce.10.cloned.1.call-start = ((), (), s32[]{:S(2)}) async-start(), calls=%async_computation.2 | async-start | bytes 131072 | tf_op jit(solution)/shard_map/psum | solution.py:107
  295.5 3.4 collective-permute-start.3
  295.6 4.9 collective-permute-start.2
  325.0 273.7 %all-reduce.12.cloned.1.call-start = ((), (), s32[]{:S(2)}) async-start(), calls=%async_computation.3 | async-start | bytes 131072 | tf_op jit(solution)/shard_map/psum | solution.py:107
  449.8 3.4 collective-permute-start.5
  449.8 4.9 collective-permute-start.4
  479.3 274.1 %all-reduce.14.cloned.1.call-start = ((), (), s32[]{:S(2)}) async-start(), calls=%async_computation.4 | async-start | bytes 131072 | tf_op jit(solution)/shard_map/psum | solution.py:107
  604.2 3.5 collective-permute-start.7
  604.2 4.9 collective-permute-start.6
Sparse Core Ops, SparseCore 0:
  14.1 123.3 all-reduce.5
  171.8 120.5 all-reduce.7
  325.2 119.2 all-reduce.9
  479.4 119.2 all-reduce.11
  634.1 119.2 all-reduce.13
where the time goes:
time: 774 us; the launch traced here: 769 us
  waiting for transfers between devices  607 us (78%)
  matrix products  72.9 us (9%)
  local copies, waits for them, and re-layouts  27.3 us (4%)
  loops' own time  25.3 us (3%)
  other arithmetic  14.7 us (2%)
  between operations  14.2 us (2%)
    psum x4, waiting for transfers between devices, local(): lax.psum(jnp.dot(image, projector, precision=highest), ('row', 'col'))  478 us
    psum x1, waiting for transfers between devices, local(): lax.psum(jnp.dot(right_side, projector, precision=highest), ('row', 'col'))  124 us
    dot_general x32, matrix products, add_slot(): jnp.einsum('rbi,boi->rbo', picked, slot_tiles, preferred_element_type=jnp...  41.8 us
    another operation x4, loops' own time, local(): lax.fori_loop(0, turns, add_slot, jnp.zeros((systems, block_rows, tile_si...  25.3 us
    gather x32, local copies, waits for them, and re-layouts, add_slot(): picked = jnp.take(blocks, wanted, axis=1)  17.5 us
  transfers between devices with their start and end apart: 13, of which 9 were waited for; matrix products, arithmetic and copies ran while one was open for 2% of the time, Pallas kernels for 0%

commit v1 on v0

v1 whole, which is shorter than its diff:
```python
import functools
import math

import jax
import jax.numpy as jnp
from jax import lax
from jax.experimental import pallas as pl
from jax.experimental.pallas import tpu as pltpu
from jax.sharding import PartitionSpec as P

SKETCH = 1024
ITERS = 4
PARTS = 3
SHIFT = 1.75
epsilon = 1e-06
MESH = pl.DeviceIdType.MESH
f32 = jnp.float32
bf16 = jnp.bfloat16


def split_parts(value):
    parts = []
    for _ in range(PARTS - 1):
        head = value.astype(bf16)
        parts.append(head)
        value = value - head.astype(f32)
    parts.append(value.astype(bf16))
    return parts


def cholesky_solve(gram, target):
    order = len(target)
    factor = {}
    inverse = []
    for column in range(order):
        diag_part = gram[column, column]
        for inner in range(column):
            diag_part = diag_part - factor[column, inner] * factor[column, inner]
        inverse.append(1.0 / jnp.sqrt(diag_part))
        for below in range(column + 1, order):
            entry = gram[below, column]
            for inner in range(column):
                entry = entry - factor[below, inner] * factor[column, inner]
            factor[below, column] = entry * inverse[column]
    forward = []
    for column in range(order):
        entry = target[column]
        for inner in range(column):
            entry = entry - factor[column, inner] * forward[inner]
        forward.append(entry * inverse[column])
    result = [None] * order
    for column in reversed(range(order)):
        entry = forward[column]
        for inner in range(column + 1, order):
            entry = entry - factor[inner, column] * result[inner]
        result[column] = entry * inverse[column]
    return result


def inner_product(a, b):
    return jnp.sum(jnp.sum(a * b, axis=0), axis=1, keepdims=True)


def nt_dot(a, b):
    return lax.dot_general(a, b, (((1,), (1,)), ((), ())), preferred_element_type=f32)


def kernel(
    rows,
    cols,
    scaling,
    columns_ref,
    counts_ref,
    aux_ref,
    right_ref,
    tiles_hbm,
    solution_ref,
    last_ref,
    hess_ref,
    tiles,
    projector,
    krylov,
    window,
    index_ref,
    halo,
    part,
    land1,
    land2,
    sketches,
    tile_sem,
    halo_send,
    halo_recv,
    send1,
    recv1,
    send2,
    recv2,
    send3,
    recv3,
):
    row = lax.axis_index("row")
    col = lax.axis_index("col")
    devices = rows * cols
    me = row * cols + col
    block_rows, slots, tile, _ = tiles.shape
    systems, width = right_ref.shape
    all_blocks = block_rows * devices
    share = SKETCH // cols
    right = lax.rem(me + 1, devices)
    left = lax.rem(me + devices - 1, devices)
    right = (lax.div(right, cols), lax.rem(right, cols))
    left = (lax.div(left, cols), lax.rem(left, cols))
    col_to = [lax.rem(col + off, cols) for off in range(cols)]
    col_from = [lax.rem(col + cols - off, cols) for off in range(cols)]
    row_to = [lax.rem(row + off, rows) for off in range(rows)]
    row_from = [lax.rem(row + rows - off, rows) for off in range(rows)]

    barrier = pltpu.get_barrier_semaphore()
    for peer in (left, right):
        pl.semaphore_signal(barrier, inc=1, device_id=peer, device_id_type=MESH)
    for off in range(1, rows):
        pl.semaphore_signal(barrier, inc=1, device_id=(row_to[off], col), device_id_type=MESH)
    for off in range(1, cols):
        pl.semaphore_signal(barrier, inc=1, device_id=(row, col_to[off]), device_id_type=MESH)

    tile_copy = pltpu.make_async_copy(tiles_hbm, tiles, tile_sem)
    tile_copy.start()

    first = me * block_rows
    for b in range(block_rows):
        for slot in range(slots):
            spot = lax.rem(columns_ref[b, slot] - first + block_rows + all_blocks, all_blocks)
            index_ref[b * slots + slot] = jnp.where(slot < counts_ref[b], spot, 3 * block_rows)
    window[3 * block_rows] = jnp.zeros(window.shape[1:], window.dtype)

    pl.semaphore_wait(barrier, rows + cols)

    def halo_copies(k):
        source = right_ref if k == 0 else krylov.at[k]
        return [
            pltpu.make_async_remote_copy(
                src_ref=source,
                dst_ref=halo.at[k, side],
                send_sem=halo_send.at[k, side],
                recv_sem=halo_recv.at[k, side],
                device_id=peer,
                device_id_type=MESH,
            )
            for side, peer in ((0, right), (1, left))
        ]

    def copy1(k, off, block):
        return pltpu.make_async_remote_copy(
            src_ref=part.at[k, block],
            dst_ref=land1.at[k, off - 1],
            send_sem=send1.at[k, off - 1],
            recv_sem=recv1.at[k, off - 1],
            device_id=(row, col_to[off]),
            device_id_type=MESH,
        )

    def copy2(k, off, source):
        return pltpu.make_async_remote_copy(
            src_ref=land2.at[k, source],
            dst_ref=land2.at[k, source],
            send_sem=send2.at[k, off - 1],
            recv_sem=recv2.at[k, off - 1],
            device_id=(row_to[off], col),
            device_id_type=MESH,
        )

    def copy3(k, off, source):
        return pltpu.make_async_remote_copy(
            src_ref=sketches.at[k, source],
            dst_ref=sketches.at[k, source],
            send_sem=send3.at[k, off - 1],
            recv_sem=recv3.at[k, off - 1],
            device_id=(row, col_to[off]),
            device_id_type=MESH,
        )

    def place(value, base):
        parts = split_parts(value)
        for b in range(block_rows):
            piece = [p[:, b * tile : (b + 1) * tile] for p in parts]
            window[base + b] = jnp.concatenate(piece, axis=0)

    def stage1(k):
        for block in range(cols):
            total = None
            for b in range(block_rows):
                term = nt_dot(
                    window[block_rows + b],
                    projector[pl.ds(block * share, share), pl.ds(b * tile, tile)],
                )
                total = term if total is None else total + term
            summed = total[(PARTS - 1) * systems :]
            for p in reversed(range(PARTS - 1)):
                summed = summed + total[p * systems : (p + 1) * systems]
            part[k, block] = summed * scaling
        for off in range(1, cols):
            copy1(k, off, col_to[off]).start()

    def stage2(k):
        for off in range(1, cols):
            copy1(k, off, 0).wait_recv()
        total = part[k, col]
        for off in range(1, cols):
            total = total + land1[k, off - 1]
        land2[k, row] = total
        for off in range(1, rows):
            copy2(k, off, row).start()

    def stage3(k):
        for off in range(1, rows):
            copy2(k, off, row_from[off]).wait_recv()
        total = land2[k, 0]
        for r in range(1, rows):
            total = total + land2[k, r]
        sketches[k, col] = total
        for off in range(1, cols):
            copy3(k, off, col).start()

    def finish(k):
        for off in range(1, cols):
            copy3(k, off, col_from[off]).wait_recv()

    for k in range(ITERS + 1):
        if k == 0:
            for copy in halo_copies(0):
                copy.start()
            krylov[0] = right_ref[...]
            diag = aux_ref[0:1, :] - SHIFT
            signed = aux_ref[1:2, :]
            targets = aux_ref[2:3, :].astype(jnp.int32)
            chunk = 64

            def build(step, carry):
                base = pl.multiple_of(step * chunk, chunk)
                spots = lax.broadcasted_iota(jnp.int32, (chunk, width), 0) + base
                projector[pl.ds(base, chunk), :] = jnp.where(
                    spots == targets, signed, 0.0
                ).astype(bf16)
                return carry

            lax.fori_loop(0, SKETCH // chunk, build, 0)
            place(right_ref[...], block_rows)
        stage1(k)
        if k >= 1:
            stage2(k - 1)
        if k >= 2:
            stage3(k - 2)
        if k == ITERS:
            break
        for copy in halo_copies(k):
            copy.wait_recv()
        place(halo[k, 0], 0)
        place(halo[k, 1], 2 * block_rows)
        if k == 0:
            tile_copy.wait()
        for b in range(block_rows):
            total = None
            for slot in range(slots):
                term = nt_dot(window[index_ref[b * slots + slot]], tiles[b, slot])
                total = term if total is None else total + term
            summed = total[(PARTS - 1) * systems :]
            for p in reversed(range(PARTS - 1)):
                summed = summed + total[p * systems : (p + 1) * systems]
            lanes = pl.ds(b * tile, tile)
            diag_b = aux_ref[0:1, lanes] - SHIFT
            krylov[k + 1, :, lanes] = diag_b * krylov[k, :, lanes] + summed
        if k + 1 < ITERS:
            for copy in halo_copies(k + 1):
                copy.start()
        place(krylov[k + 1], block_rows)

    coords = []
    sketched = []
    gram = {}
    hess = {}

    def arnoldi(j):
        spread = [None] * (j + 1)
        for i in range(j):
            spread[i] = SHIFT * coords[j - 1][i]
        for i in range(j):
            moved = coords[j - 1][i]
            spread[i + 1] = moved if spread[i + 1] is None else spread[i + 1] + moved
        image = spread[0] * sketches[0]
        for i in range(1, j + 1):
            image = image + spread[i] * sketches[i]
        target = [inner_product(q, image) for q in sketched]
        coeffs = cholesky_solve(gram, target)
        for i in range(j):
            image = image - coeffs[i] * sketched[i]
            for m in range(i + 1):
                spread[m] = spread[m] - coeffs[i] * coords[i][m]
        square = inner_product(image, image) + epsilon
        norm = jnp.sqrt(square)
        scale = 1.0 / norm
        for i in range(j):
            hess[i, j - 1] = coeffs[i]
        hess[j, j - 1] = norm
        coords.append([entry * scale for entry in spread])
        if j < ITERS:
            add_sketched(image * scale)

    def add_sketched(q):
        sketched.append(q)
        n = len(sketched)
        for i in range(n):
            gram[n - 1, i] = inner_product(q, sketched[i])

    finish(0)
    start = sketches[0]
    beta = jnp.sqrt(inner_product(start, start) + epsilon)
    coords.append([1.0 / beta])
    add_sketched(start * coords[0][0])
    finish(1)
    arnoldi(1)
    stage2(ITERS)
    stage3(ITERS - 1)
    finish(2)
    arnoldi(2)
    stage3(ITERS)
    finish(3)
    arnoldi(3)
    finish(4)
    arnoldi(4)

    lane = lax.broadcasted_iota(jnp.int32, hess_ref.shape, 1)
    packed = jnp.zeros(hess_ref.shape, f32)
    for (i, j), value in hess.items():
        packed = jnp.where(lane == i * ITERS + j, value, packed)
    hess_ref[...] = packed

    normal = {}
    for m in range(ITERS):
        for n in range(m + 1):
            entry = None
            for i in range(min(m, n) + 2):
                term = hess[i, m] * hess[i, n]
                entry = term if entry is None else entry + term
            normal[m, n] = entry
    weights = cholesky_solve(normal, [beta * hess[0, n] for n in range(ITERS)])
    mixed = []
    for m in range(ITERS):
        entry = None
        for i in range(m, ITERS):
            term = weights[i] * coords[i][m]
            entry = term if entry is None else entry + term
        mixed.append(entry)
    out = mixed[0] * krylov[0]
    for m in range(1, ITERS):
        out = out + mixed[m] * krylov[m]
    solution_ref[...] = out
    out = coords[ITERS][0] * krylov[0]
    for m in range(1, ITERS + 1):
        out = out + coords[ITERS][m] * krylov[m]
    last_ref[...] = out

    for k in range(ITERS + 1):
        if k < ITERS:
            for copy in halo_copies(k):
                copy.wait_send()
        for off in range(1, cols):
            copy1(k, off, col_to[off]).wait_send()
            copy3(k, off, col).wait_send()
        for off in range(1, rows):
            copy2(k, off, row).wait_send()


def local(
    rows, cols, tile_values, block_columns, tile_counts, diagonal, sketch_rows, sketch_signs, right_side
):
    block_rows, _, tile, _ = tile_values.shape
    systems, width = right_side.shape
    scaling = 1.0 / math.sqrt(width * rows * cols)
    share = SKETCH // cols
    vectors = ITERS + 1
    aux = jnp.stack(
        [diagonal, (2 * sketch_signs - 1).astype(f32), sketch_rows.astype(f32)], axis=0
    )
    vmem = pl.BlockSpec(memory_space=pltpu.VMEM)
    smem = pl.BlockSpec(memory_space=pltpu.SMEM)
    dma = pltpu.SemaphoreType.DMA
    iterate, last, packed = pl.pallas_call(
        functools.partial(kernel, rows, cols, scaling),
        out_shape=(
            jax.ShapeDtypeStruct((systems, width), f32),
            jax.ShapeDtypeStruct((systems, width), f32),
            jax.ShapeDtypeStruct((systems, 128), f32),
        ),
        in_specs=[smem, smem, vmem, vmem, pl.BlockSpec(memory_space=pl.ANY)],
        out_specs=(vmem, vmem, vmem),
        scratch_shapes=[
            pltpu.VMEM(tile_values.shape, bf16),
            pltpu.VMEM((SKETCH, width), bf16),
            pltpu.VMEM((vectors, systems, width), f32),
            pltpu.VMEM((3 * block_rows + 1, PARTS * systems, tile), bf16),
            pltpu.SMEM((tile_values.shape[0] * tile_values.shape[1],), jnp.int32),
            pltpu.VMEM((ITERS, 2, systems, width), f32),
            pltpu.VMEM((vectors, cols, systems, share), f32),
            pltpu.VMEM((vectors, cols - 1, systems, share), f32),
            pltpu.VMEM((vectors, rows, systems, share), f32),
            pltpu.VMEM((vectors, cols, systems, share), f32),
            dma,
            dma((ITERS, 2)),
            dma((ITERS, 2)),
            dma((vectors, cols - 1)),
            dma((vectors, cols - 1)),
            dma((vectors, rows - 1)),
            dma((vectors, rows - 1)),
            dma((vectors, cols - 1)),
            dma((vectors, cols - 1)),
        ],
        compiler_params=pltpu.CompilerParams(
            collective_id=0, has_side_effects=True, vmem_limit_bytes=48 * 1024 * 1024
        ),
    )(block_columns, tile_counts, aux, right_side, tile_values)
    hessenberg = packed[:, : (ITERS + 1) * ITERS].reshape(systems, ITERS + 1, ITERS)
    return iterate, last, hessenberg


def solution(mesh):
    spec = P(("row", "col"))
    in_specs = (
        P(("row", "col"), None, None, None),
        P(("row", "col"), None),
        spec,
        spec,
        spec,
        spec,
        P(None, ("row", "col")),
    )
    out_specs = (P(None, ("row", "col")), P(None, ("row", "col")), P())
    body = functools.partial(local, mesh.shape["row"], mesh.shape["col"])
    return jax.shard_map(body, mesh=mesh, in_specs=in_specs, out_specs=out_specs, check_vma=False)
```

time: 774 us -> 51.2 us (0.07)
  the two profiles are of different devices: /device:TPU:1 before, /device:TPU:29 now
where the time goes in v1:
time: 51.2 us; the launch traced here: 50.9 us
  Pallas kernels  41.9 us (82%)
  local copies, waits for them, and re-layouts  6.31 us (12%)
  other arithmetic  2.08 us (4%)
  between operations  0.65 us (1%)
    pallas_call x1, Pallas kernels, local(): pl.pallas_call(functools.partial(kernel, rows, cols, scaling), out_shape=...  41.9 us
    unnamed x10, local copies, waits for them, and re-layouts  5.62 us

profile of v1, /device:TPU:29, one launch (start us, length us, event | category | flops | bytes accessed | tf_op | source)
XLA Modules:
  0.0 50.9 jit_solution(10038009896454795746)
XLA Ops:
  0.6 0.7 %add_convert_fusion = f32[1024]{0:T(1024)S(1)} fusion(s32[1024]{0:T(1024)} %param.12), kind=kLoop, calls=%fused_computation.1 | loop fusion | flops 3072 | bytes 8192 | tf_op jit(solution)/shard_map/convert_element_type | solution.py:381
  1.3 0.7 %convert_element_type.7 = f32[1024]{0:T(1024)S(1)} convert(s32[1024]{0:T(1024)} %param.11) | non-fusion elementwise | flops 1024 | bytes 8192 | tf_op jit(solution)/shard_map/convert_element_type | solution.py:381
  2.0 0.7 %pad_maximum_fusion.aux_ref = f32[3,1024]{1,0:T(4,128)S(1)} fusion(f32[1,1024]{1,0:T(1,128)S(1)} %bitcast.8, f32[1,1024]{1,0:T(1,128)S(1)} %bitcast.7, f32[1,1024]{1,0:T(1,128)} %bitcast.9), kind=kLoop, calls=%fused_computation | loop fusion | flops 6144 | bytes 24576 | tf_op jit(solution)/shard_map/stack | solution.py:380
  2.7 0.0 copy-start
  2.7 2.2 %copy-done = bf16[4,8,256,256]{3,2,1,0:T(8,128)(2,1)S(1)} copy-done((bf16[4,8,256,256]{3,2,1,0:T(8,128)(2,1)S(1)}, bf16[4,8,256,256]{3,2,1,0:T(8,128)(2,1)}, u32[]{:S(2)}) %copy-start) | copy-done | bytes 4194328
  4.9 0.0 copy-start.1
  4.9 0.8 %copy-done.1 = f32[16,1024]{1,0:T(8,128)S(1)} copy-done((f32[16,1024]{1,0:T(8,128)S(1)}, f32[16,1024]{1,0:T(8,128)}, u32[]{:S(2)}) %copy-start.1) | copy-done | bytes 65560
  5.7 0.0 copy-start.2
  5.7 0.7 %copy-done.2 = s32[4,8]{1,0:T(4,128)S(1)} copy-done((s32[4,8]{1,0:T(4,128)S(1)}, s32[4,8]{1,0:T(4,128)}, u32[]{:S(2)}) %copy-start.2) | copy-done | bytes 152
  6.4 0.0 copy-start.3
  6.4 0.7 %copy-done.3 = s32[4]{0:T(128)S(1)} copy-done((s32[4]{0:T(128)S(1)}, s32[4]{0:T(128)}, u32[]{:S(2)}) %copy-start.3) | copy-done | bytes 40
  7.1 41.9 %shard_map.94 = (f32[16,1024]{1,0:T(8,128)S(1)}, f32[16,1024]{1,0:T(8,128)S(1)}, f32[16,128]{1,0:T(8,128)S(1)}) custom-call(s32[4,8]{1,0:T(4,128)S(1)} %copy-done.2, s32[4]{0:T(128)S(1)} %copy-done.3, f32[3,1024]{1,0:T(4,128)S(1)} %pad_maximum_fusion.aux_ref, f32[16,1024]{1,0:T(8,128)S(1)} %copy-done.1, bf16[4,8,256,256]{3,2,1,0:T(8,128)(2,1)S(1)} %copy-done), custom_call_target="tpu_custom_call" | custom-call | tf_op jit(solution)/shard_map/pallas_call | solution.py:386
  49.0 0.1 copy.11
  49.1 0.6 %reshape.9 = f32[16,5,4]{0,2,1:T(4,128)} reshape(f32[16,20]{0,1:T(8,128)S(1)} %copy.11) | data formatting | bytes 2560 | tf_op jit(solution)/shard_map/reshape | solution.py:420
  49.7 0.6 %copy.14 = f32[16,1024]{1,0:T(8,128)} copy(f32[16,1024]{1,0:T(8,128)S(1)} %get-tuple-element.15) | data formatting | bytes 131072
  50.3 0.6 %copy.15 = f32[16,1024]{1,0:T(8,128)} copy(f32[16,1024]{1,0:T(8,128)S(1)} %get-tuple-element.16) | data formatting | bytes 131072
Async XLA Ops:
  2.7 2.2 %copy-start = (bf16[4,8,256,256]{3,2,1,0:T(8,128)(2,1)S(1)}, bf16[4,8,256,256]{3,2,1,0:T(8,128)(2,1)}, u32[]{:S(2)}) copy-start(bf16[4,8,256,256]{3,2,1,0:T(8,128)(2,1)} %tiles_hbm.1) | copy-start | bytes 12582916
  4.9 0.8 %copy-start.1 = (f32[16,1024]{1,0:T(8,128)S(1)}, f32[16,1024]{1,0:T(8,128)}, u32[]{:S(2)}) copy-start(f32[16,1024]{1,0:T(8,128)} %right_ref.1) | copy-start | bytes 196612
  5.7 0.7 %copy-start.2 = (s32[4,8]{1,0:T(4,128)S(1)}, s32[4,8]{1,0:T(4,128)}, u32[]{:S(2)}) copy-start(s32[4,8]{1,0:T(4,128)} %columns_ref.1) | copy-start | bytes 388
  6.4 0.7 %copy-start.3 = (s32[4]{0:T(128)S(1)}, s32[4]{0:T(128)}, u32[]{:S(2)}) copy-start(s32[4]{0:T(128)} %counts_ref.1) | copy-start | bytes 52

commit v2 on v1

v2 whole, which is shorter than its diff:
```python
import functools
import math

import jax
import jax.numpy as jnp
from jax import lax
from jax.experimental import pallas as pl
from jax.experimental.pallas import tpu as pltpu
from jax.sharding import PartitionSpec as P

SKETCH = 1024
ITERS = 4
PARTS = 3
SHIFT = 1.75
epsilon = 1e-06
MESH = pl.DeviceIdType.MESH
f32 = jnp.float32
bf16 = jnp.bfloat16


def split_parts(value):
    parts = []
    for _ in range(PARTS - 1):
        head = value.astype(bf16)
        parts.append(head)
        value = value - head.astype(f32)
    parts.append(value.astype(bf16))
    return parts


def extend_factor(factor, inverse, entries):
    row = len(inverse)
    for column in range(row):
        entry = entries[column]
        for inner in range(column):
            entry = entry - factor[row, inner] * factor[column, inner]
        factor[row, column] = entry * inverse[column]
    diag_part = entries[row]
    for inner in range(row):
        diag_part = diag_part - factor[row, inner] * factor[row, inner]
    inverse.append(1.0 / jnp.sqrt(diag_part))


def factor_solve(factor, inverse, target):
    order = len(target)
    forward = []
    for column in range(order):
        entry = target[column]
        for inner in range(column):
            entry = entry - factor[column, inner] * forward[inner]
        forward.append(entry * inverse[column])
    result = [None] * order
    for column in reversed(range(order)):
        entry = forward[column]
        for inner in range(column + 1, order):
            entry = entry - factor[inner, column] * result[inner]
        result[column] = entry * inverse[column]
    return result


def inner_product(a, b):
    return jnp.sum(jnp.sum(a * b, axis=0), axis=1, keepdims=True)


def nt_dot(a, b):
    return lax.dot_general(a, b, (((1,), (1,)), ((), ())), preferred_element_type=f32)


def kernel(
    rows,
    cols,
    scaling,
    columns_hbm,
    counts_hbm,
    diag_hbm,
    rows_hbm,
    signs_hbm,
    right_hbm,
    tiles_hbm,
    solution_ref,
    last_ref,
    hess_ref,
    columns_ref,
    counts_ref,
    diag_ref,
    rows_ref,
    signs_ref,
    tiles,
    projector,
    krylov,
    window,
    index_ref,
    halo,
    part,
    land1,
    land2,
    sketches,
    load_sem,
    halo_send,
    halo_recv,
    send1,
    recv1,
    send2,
    recv2,
    send3,
    recv3,
):
    row = lax.axis_index("row")
    col = lax.axis_index("col")
    devices = rows * cols
    me = row * cols + col
    block_rows, slots, tile, _ = tiles.shape
    systems, width = right_hbm.shape
    all_blocks = block_rows * devices
    share = SKETCH // cols
    right = lax.rem(me + 1, devices)
    left = lax.rem(me + devices - 1, devices)
    right = (lax.div(right, cols), lax.rem(right, cols))
    left = (lax.div(left, cols), lax.rem(left, cols))
    col_to = [lax.rem(col + off, cols) for off in range(cols)]
    col_from = [lax.rem(col + cols - off, cols) for off in range(cols)]
    row_to = [lax.rem(row + off, rows) for off in range(rows)]
    row_from = [lax.rem(row + rows - off, rows) for off in range(rows)]

    barrier = pltpu.get_barrier_semaphore()
    for peer in (left, right):
        pl.semaphore_signal(barrier, inc=1, device_id=peer, device_id_type=MESH)
    for off in range(1, rows):
        pl.semaphore_signal(barrier, inc=1, device_id=(row_to[off], col), device_id_type=MESH)
    for off in range(1, cols):
        pl.semaphore_signal(barrier, inc=1, device_id=(row, col_to[off]), device_id_type=MESH)

    loads = [
        pltpu.make_async_copy(source, target, load_sem.at[n])
        for n, (source, target) in enumerate(
            [
                (rows_hbm, rows_ref),
                (signs_hbm, signs_ref),
                (columns_hbm, columns_ref),
                (counts_hbm, counts_ref),
                (diag_hbm, diag_ref),
            ]
            + [
                (right_hbm.at[:, pl.ds(b * tile, tile)], krylov.at[0, b])
                for b in range(block_rows)
            ]
            + [(tiles_hbm, tiles)]
        )
    ]
    for load in loads:
        load.start()
    for load in loads[:4]:
        load.wait()

    first = me * block_rows
    for b in range(block_rows):
        for slot in range(slots):
            spot = lax.rem(columns_ref[b, slot] - first + block_rows + all_blocks, all_blocks)
            index_ref[b * slots + slot] = jnp.where(slot < counts_ref[b], spot, 3 * block_rows)
    window[3 * block_rows] = jnp.zeros(window.shape[1:], window.dtype)

    signed = (2 * signs_ref[...] - 1).astype(f32)
    targets = rows_ref[...]
    chunk = 64

    def build(step, carry):
        base = pl.multiple_of(step * chunk, chunk)
        spots = lax.broadcasted_iota(jnp.int32, (chunk, width), 0) + base
        projector[pl.ds(base, chunk), :] = jnp.where(spots == targets, signed, 0.0).astype(bf16)
        return carry

    lax.fori_loop(0, SKETCH // chunk, build, 0)
    for load in loads[4:-1]:
        load.wait()
    pl.semaphore_wait(barrier, rows + cols)

    def halo_copies(k, b):
        return [
            pltpu.make_async_remote_copy(
                src_ref=krylov.at[k, b],
                dst_ref=halo.at[k, side, b],
                send_sem=halo_send.at[k, side, b],
                recv_sem=halo_recv.at[k, side, b],
                device_id=peer,
                device_id_type=MESH,
            )
            for side, peer in ((0, right), (1, left))
        ]

    def copy1(k, off, block):
        return pltpu.make_async_remote_copy(
            src_ref=part.at[k, block],
            dst_ref=land1.at[k, off - 1],
            send_sem=send1.at[k, off - 1],
            recv_sem=recv1.at[k, off - 1],
            device_id=(row, col_to[off]),
            device_id_type=MESH,
        )

    def copy2(k, off, source):
        return pltpu.make_async_remote_copy(
            src_ref=land2.at[k, source],
            dst_ref=land2.at[k, source],
            send_sem=send2.at[k, off - 1],
            recv_sem=recv2.at[k, off - 1],
            device_id=(row_to[off], col),
            device_id_type=MESH,
        )

    def copy3(k, off, source):
        return pltpu.make_async_remote_copy(
            src_ref=sketches.at[k, source],
            dst_ref=sketches.at[k, source],
            send_sem=send3.at[k, off - 1],
            recv_sem=recv3.at[k, off - 1],
            device_id=(row, col_to[off]),
            device_id_type=MESH,
        )

    def place(value, spot):
        window[spot] = jnp.concatenate(split_parts(value), axis=0)

    def stage1(k):
        for block in range(cols):
            total = None
            for b in range(block_rows):
                term = nt_dot(
                    window[block_rows + b],
                    projector[pl.ds(block * share, share), pl.ds(b * tile, tile)],
                )
                total = term if total is None else total + term
            summed = total[(PARTS - 1) * systems :]
            for p in reversed(range(PARTS - 1)):
                summed = summed + total[p * systems : (p + 1) * systems]
            part[k, block] = summed * scaling
        for off in range(1, cols):
            copy1(k, off, col_to[off]).start()

    def stage2(k):
        for off in range(1, cols):
            copy1(k, off, 0).wait_recv()
        total = part[k, col]
        for off in range(1, cols):
            total = total + land1[k, off - 1]
        land2[k, row] = total
        for off in range(1, rows):
            copy2(k, off, row).start()

    def stage3(k):
        for off in range(1, rows):
            copy2(k, off, row_from[off]).wait_recv()
        total = land2[k, 0]
        for r in range(1, rows):
            total = total + land2[k, r]
        sketches[k, col] = total
        for off in range(1, cols):
            copy3(k, off, col).start()

    def finish(k):
        for off in range(1, cols):
            copy3(k, off, col_from[off]).wait_recv()

    coords = []
    sketched = []
    factor, inverse = {}, []
    hess = {}
    normal, normal_inverse = {}, []

    def spread_of(j):
        spread = [SHIFT * entry for entry in coords[j - 1]] + [None]
        for i in range(j):
            moved = coords[j - 1][i]
            spread[i + 1] = moved if spread[i + 1] is None else spread[i + 1] + moved
        image = spread[0] * sketches[0]
        for i in range(1, j):
            image = image + spread[i] * sketches[i]
        return spread, image

    def arnoldi(j, prepared):
        spread, image = prepared
        image = image + spread[j] * sketches[j]
        coeffs = factor_solve(factor, inverse, [inner_product(q, image) for q in sketched])
        for i in range(j):
            image = image - coeffs[i] * sketched[i]
            for m in range(i + 1):
                spread[m] = spread[m] - coeffs[i] * coords[i][m]
        norm = jnp.sqrt(inner_product(image, image) + epsilon)
        scale = 1.0 / norm
        for i in range(j):
            hess[i, j - 1] = coeffs[i]
        hess[j, j - 1] = norm
        coords.append([entry * scale for entry in spread])
        if j < ITERS:
            add_sketched(image * scale)
        entries = []
        for n in range(j):
            entry = None
            for i in range(n + 2):
                term = hess[i, j - 1] * hess[i, n]
                entry = term if entry is None else entry + term
            entries.append(entry)
        extend_factor(normal, normal_inverse, entries)

    def add_sketched(q):
        sketched.append(q)
        extend_factor(factor, inverse, [inner_product(q, other) for other in sketched])

    for b in range(block_rows):
        for copy in halo_copies(0, b):
            copy.start()
    for b in range(block_rows):
        place(krylov[0, b], block_rows + b)
    beta = None
    for k in range(ITERS):
        stage1(k)
        if k >= 1:
            stage3(k - 1)
        if k == 2:
            finish(0)
            start = sketches[0]
            beta = jnp.sqrt(inner_product(start, start) + epsilon)
            coords.append([1.0 / beta])
            add_sketched(start * coords[0][0])
        if k >= 3:
            finish(k - 2)
            arnoldi(k - 2, spread_of(k - 2))
        stage2(k)
        for b in range(block_rows):
            for copy in halo_copies(k, b):
                copy.wait_recv()
            place(halo[k, 0, b], b)
            place(halo[k, 1, b], 2 * block_rows + b)
        if k == 0:
            loads[-1].wait()
        for b in range(block_rows):
            total = None
            for slot in range(slots):
                term = nt_dot(window[index_ref[b * slots + slot]], tiles[b, slot])
                total = term if total is None else total + term
            summed = total[(PARTS - 1) * systems :]
            for p in reversed(range(PARTS - 1)):
                summed = summed + total[p * systems : (p + 1) * systems]
            diag_b = diag_ref[0:1, pl.ds(b * tile, tile)] - SHIFT
            krylov[k + 1, b] = diag_b * krylov[k, b] + summed
            if k + 1 < ITERS:
                for copy in halo_copies(k + 1, b):
                    copy.start()
        for b in range(block_rows):
            place(krylov[k + 1, b], block_rows + b)
    stage1(ITERS)
    stage3(ITERS - 1)
    finish(ITERS - 2)
    arnoldi(ITERS - 2, spread_of(ITERS - 2))
    stage2(ITERS)
    finish(ITERS - 1)
    arnoldi(ITERS - 1, spread_of(ITERS - 1))
    prepared = spread_of(ITERS)
    stage3(ITERS)
    finish(ITERS)
    arnoldi(ITERS, prepared)

    lane = lax.broadcasted_iota(jnp.int32, (systems, 128), 1)
    packed = jnp.zeros((systems, 128), f32)
    for (i, j), value in hess.items():
        packed = jnp.where(lane == i * ITERS + j, value, packed)
    turned = packed.T
    for i in range(ITERS + 1):
        hess_ref[i] = turned[i * ITERS : (i + 1) * ITERS, :]

    weights = factor_solve(normal, normal_inverse, [beta * hess[0, n] for n in range(ITERS)])
    mixed = []
    for m in range(ITERS):
        entry = None
        for i in range(m, ITERS):
            term = weights[i] * coords[i][m]
            entry = term if entry is None else entry + term
        mixed.append(entry)
    for b in range(block_rows):
        lanes = pl.ds(b * tile, tile)
        out = mixed[0] * krylov[0, b]
        for m in range(1, ITERS):
            out = out + mixed[m] * krylov[m, b]
        solution_ref[:, lanes] = out
        out = coords[ITERS][0] * krylov[0, b]
        for m in range(1, ITERS + 1):
            out = out + coords[ITERS][m] * krylov[m, b]
        last_ref[:, lanes] = out

    for k in range(ITERS + 1):
        if k < ITERS:
            for b in range(block_rows):
                for copy in halo_copies(k, b):
                    copy.wait_send()
        for off in range(1, cols):
            copy1(k, off, col_to[off]).wait_send()
            copy3(k, off, col).wait_send()
        for off in range(1, rows):
            copy2(k, off, row).wait_send()


def local(
    rows, cols, tile_values, block_columns, tile_counts, diagonal, sketch_rows, sketch_signs, right_side
):
    block_rows, _, tile, _ = tile_values.shape
    systems, width = right_side.shape
    scaling = 1.0 / math.sqrt(width * rows * cols)
    share = SKETCH // cols
    vectors = ITERS + 1
    vmem = pl.BlockSpec(memory_space=pltpu.VMEM)
    hbm = pl.BlockSpec(memory_space=pltpu.HBM)
    dma = pltpu.SemaphoreType.DMA
    iterate, last, hessenberg = pl.pallas_call(
        functools.partial(kernel, rows, cols, scaling),
        out_shape=(
            pltpu.VMEM((systems, width), f32),
            pltpu.VMEM((systems, width), f32),
            pltpu.VMEM((ITERS + 1, ITERS, systems), f32),
        ),
        in_specs=[hbm] * 7,
        out_specs=(vmem, vmem, vmem),
        scratch_shapes=[
            pltpu.SMEM(block_columns.shape, jnp.int32),
            pltpu.SMEM(tile_counts.shape, jnp.int32),
            pltpu.VMEM((1, width), f32),
            pltpu.VMEM((1, width), jnp.int32),
            pltpu.VMEM((1, width), jnp.int32),
            pltpu.VMEM(tile_values.shape, bf16),
            pltpu.VMEM((SKETCH, width), bf16),
            pltpu.VMEM((vectors, block_rows, systems, tile), f32),
            pltpu.VMEM((3 * block_rows + 1, PARTS * systems, tile), bf16),
            pltpu.SMEM((tile_values.shape[0] * tile_values.shape[1],), jnp.int32),
            pltpu.VMEM((ITERS, 2, block_rows, systems, tile), f32),
            pltpu.VMEM((vectors, cols, systems, share), f32),
            pltpu.VMEM((vectors, cols - 1, systems, share), f32),
            pltpu.VMEM((vectors, rows, systems, share), f32),
            pltpu.VMEM((vectors, cols, systems, share), f32),
            dma((block_rows + 6,)),
            dma((ITERS, 2, block_rows)),
            dma((ITERS, 2, block_rows)),
            dma((vectors, cols - 1)),
            dma((vectors, cols - 1)),
            dma((vectors, rows - 1)),
            dma((vectors, rows - 1)),
            dma((vectors, cols - 1)),
            dma((vectors, cols - 1)),
        ],
        compiler_params=pltpu.CompilerParams(
            collective_id=0, has_side_effects=True, vmem_limit_bytes=67043328 - 160 * 1024
        ),
    )(
        block_columns,
        tile_counts,
        diagonal.reshape(1, width),
        sketch_rows.reshape(1, width),
        sketch_signs.reshape(1, width),
        right_side,
        tile_values,
    )
    return iterate, last, jnp.transpose(hessenberg, (2, 0, 1))


def solution(mesh):
    spec = P(("row", "col"))
    in_specs = (
        P(("row", "col"), None, None, None),
        P(("row", "col"), None),
        spec,
        spec,
        spec,
        spec,
        P(None, ("row", "col")),
    )
    out_specs = (P(None, ("row", "col")), P(None, ("row", "col")), P())
    body = functools.partial(local, mesh.shape["row"], mesh.shape["col"])
    return jax.shard_map(body, mesh=mesh, in_specs=in_specs, out_specs=out_specs, check_vma=False)
```

time: 51.2 us -> 47.7 us (0.932)
  the two profiles are of different devices: /device:TPU:29 before, /device:TPU:1 now
where the time goes in v2:
time: 47.7 us; the launch traced here: 47.1 us
  Pallas kernels  44.6 us (94%)
  local copies, waits for them, and re-layouts  1.86 us (4%)
  between operations  0.64 us (1%)
    pallas_call x1, Pallas kernels, local(): pl.pallas_call(functools.partial(kernel, rows, cols, scaling), out_shape=...  44.6 us
    unnamed x3, local copies, waits for them, and re-layouts  1.86 us

profile of v2, /device:TPU:1, one launch (start us, length us, event | category | flops | bytes accessed | tf_op | source)
XLA Modules:
  0.0 47.1 jit_solution(13307700867137716764)
XLA Ops:
  0.6 44.6 %shard_map.94 = (f32[16,1024]{1,0:T(8,128)S(1)}, f32[16,1024]{1,0:T(8,128)S(1)}, f32[5,4,16]{2,1,0:T(4,128)S(1)}) custom-call(s32[4,8]{1,0:T(4,128)} %columns_hbm.1, s32[4]{0:T(128)} %counts_hbm.1, f32[1,1024]{1,0:T(1,128)} %bitcast.5, s32[1,1024]{1,0:T(1,128)} %bitcast.6, s32[1,1024]{1,0:T(1,128)} %bitcast.7, f32[16,1024]{1,0:T(8,128)} %right_hbm.1, ...), custom_call_target="tpu_custom_call" | custom-call | tf_op jit(solution)/shard_map/pallas_call | solution.py:412
  45.3 0.6 %copy.13 = f32[16,1024]{1,0:T(8,128)} copy(f32[16,1024]{1,0:T(8,128)S(1)} %get-tuple-element.9) | data formatting | bytes 131072
  45.9 0.6 %copy.15 = f32[16,5,4]{0,2,1:T(4,128)} copy(f32[16,5,4]{0,2,1:T(4,128)S(1)} %bitcast.4) | data formatting | bytes 2560
  46.5 0.6 %copy.14 = f32[16,1024]{1,0:T(8,128)} copy(f32[16,1024]{1,0:T(8,128)S(1)} %get-tuple-element.10) | data formatting | bytes 131072
